TPU v7x, 128 devices: a whole 4x4x4 slice. The times are simulated.
128 devices in a mesh: data: 1, dap2: 16 (over z, y), dap: 8 (over x, core).
Axes of the slice: x: 4, y: 4, z: 4, core: 2. Of those that a mesh axis runs over, the one named last changes fastest.
Arguments:
- pair_rep: float32 [1024, 1024, 128], P(('data', 'dap2', 'dap'))
- pair_mask: int32 [1024, 1024], P(('data', 'dap2', 'dap'))
- norm_gain: bfloat16 [2, 128], replicated
- norm_bias: bfloat16 [2, 128], replicated
- w_proj: bfloat16 [2, 128, 512], replicated
- w_gate: bfloat16 [2, 128, 128], replicated
- post_gain: bfloat16 [2, 128], replicated
- post_bias: bfloat16 [2, 128], replicated
- w_out: bfloat16 [2, 128, 128], replicated
Outputs:
- output: float32 [1024, 1024, 128], P(('data', 'dap2', 'dap'))
All inputs are finite; a program needn't handle non-finite values.
Results may differ from a plain program's by a relative error of at most 0.00102608.
Values are sent between devices in bfloat16 or wider.
A program may use at most 1 GiB of HBM per device.

v0:
```python
import jax
import jax.numpy as jnp
from jax import lax
from jax.sharding import PartitionSpec as P

NORM_EPS = 1e-5
GROUP_AXES = ('dap2', 'dap')
ROW_SPEC = P(('data', 'dap2', 'dap'), None, None)
MASK_SPEC = P(('data', 'dap2', 'dap'), None)


def layer_norm(values, scale_vec, shift_vec, norm_axis):
    row_mean = jnp.mean(values, axis=norm_axis, keepdims=True)
    centered = values - row_mean
    row_var = jnp.mean(centered * centered, axis=norm_axis, keepdims=True)
    scaled = centered * lax.rsqrt(row_var + NORM_EPS)
    return (scaled * scale_vec.astype(jnp.float32) + shift_vec.astype(jnp.float32)).astype(jnp.bfloat16)


def gated_side(normed, w_pair, keep_mask, form):
    channels = w_pair.shape[1] // 2
    projected = jnp.einsum(form, normed, w_pair, preferred_element_type=jnp.float32)
    return (keep_mask * jax.nn.sigmoid(projected[channels:]) * projected[:channels]).astype(jnp.bfloat16)


def finish(pair_rows, normed, mixed_sum, post_gain, post_bias, w_gate, w_out):
    post_norm = layer_norm(mixed_sum, post_gain[:, None, None], post_bias[:, None, None], 0)
    update = jnp.einsum('cij,cd->ijd', post_norm, w_out, preferred_element_type=jnp.float32)
    gate_pre = jnp.einsum('ijd,de->ije', normed, w_gate, preferred_element_type=jnp.float32)
    return pair_rows + jax.nn.sigmoid(gate_pre) * update


def solution(mesh):
    def local_step(pair_rows, mask_rows, norm_gain, norm_bias, w_proj, w_gate, post_gain, post_bias, w_out):
        channels = w_out.shape[1]
        keep_mask = mask_rows.astype(jnp.float32)
        normed = layer_norm(pair_rows, norm_gain[0], norm_bias[0], -1)
        side_a = gated_side(normed, w_proj[0, :, :2 * channels], keep_mask, 'ikd,de->eik')
        side_b = gated_side(normed, w_proj[0, :, 2 * channels:], keep_mask, 'jkd,de->ejk')
        full_b = lax.all_gather(side_b, GROUP_AXES, axis=1, tiled=True)
        mixed_sum = jnp.einsum('cik,cjk->cij', side_a, full_b, preferred_element_type=jnp.float32)
        pair_mid = finish(pair_rows, normed, mixed_sum, post_gain[0], post_bias[0], w_gate[0], w_out[0])
        normed = layer_norm(pair_mid, norm_gain[1], norm_bias[1], -1)
        side_a = gated_side(normed, w_proj[1, :, :2 * channels], keep_mask, 'kid,de->eki')
        side_b = gated_side(normed, w_proj[1, :, 2 * channels:], keep_mask, 'kjd,de->ekj')
        cols_a = lax.all_to_all(side_a, GROUP_AXES, 2, 1, tiled=True)
        full_b = lax.all_gather(side_b, GROUP_AXES, axis=1, tiled=True)
        mixed_sum = jnp.einsum('cki,ckj->cij', cols_a, full_b, preferred_element_type=jnp.float32)
        return finish(pair_mid, normed, mixed_sum, post_gain[1], post_bias[1], w_gate[1], w_out[1])

    replicated = P()
    return jax.shard_map(local_step, mesh=mesh,
                         in_specs=(ROW_SPEC, MASK_SPEC) + (replicated,) * 7,
                         out_specs=ROW_SPEC, check_vma=False)
```

profile of v0, /device:TPU:1, one launch (start us, length us, event | category | flops | bytes accessed | tf_op | source)
XLA Modules:
  0.0 2209.0 jit_solution(15447610437875182096)
XLA Ops:
  6.5 0.0 copy-start.10
  6.5 0.0 all-gather.3.cloned.1.call-start
  6.5 3.4 reduce_sum.72
  9.9 0.0 copy-start
  9.9 4.1 multiply_reduce_fusion.3
  14.1 0.0 copy-start.6
  14.1 0.0 copy-done.10
  14.1 0.0 copy-done.9
  14.1 0.0 copy-done
  14.1 3.0 add_convert_fusion.3
  17.1 0.0 copy-done.6
  17.1 1.2 convolution_bitcast_fusion.2
  18.3 0.0 copy-start.8
  18.4 1.2 convolution_bitcast_fusion.3
  19.6 0.0 copy-done.8
  19.6 3.8 fusion.14
  23.4 3.9 copy.60
  27.3 0.0 all-gather.3.cloned.1.call-update
  27.3 0.0 all-gather.5.cloned.1.call-start
  27.4 5.3 copy.65
  32.7 4.2 copy.61
  37.0 0.0 copy-done.11
  37.0 0.0 copy-done.12
  37.0 0.5 bitcast_convert_fusion
  37.5 0.0 copy-done.7
  37.5 2.7 fusion.35
  40.2 516.6 %all-gather.3.cloned.1.call-done = bf16[128,1024,1024]{2,0,1:T(8,128)(2,1)} async-done(((bf16[128,8,1024]{2,0,1:T(8,128)(2,1)}), bf16[128,1024,1024]{2,0,1:T(8,128)(2,1)}) %all-gather.3.cloned.1.call-update) | async-done | bytes 268435456 | tf_op jit(solution)/shard_map/all_gather | solution.py:40
  556.8 633.7 %fusion.44 = (f32[8,1024]{1,0:T(8,128)S(1)}, f32[128,8,1024]{2,1,0:T(8,128)}) fusion(bf16[128,8,1024]{2,1,0:T(8,128)(2,1)} %copy.61, bf16[128,1024,1024]{2,0,1:T(8,128)(2,1)} %all-gather.3.cloned.1.call-done), kind=kOutput, calls=%fused_computation.82 | convolution fusion | flops 2148524032 | bytes 274759680 | tf_op jit(solution)/shard_map/cik,cjk->cij/dot_general | solution.py:41
  1190.5 0.0 copy-start.2
  1190.6 2.8 multiply_reduce_fusion.2
  1193.4 0.0 copy-start.15
  1193.4 0.6 copy-done.2
  1194.0 0.6 add_convert_fusion.2
  1194.6 1.1 copy-done.5
  1195.7 0.0 copy-done.15
  1195.7 5.5 fusion.45
  1201.3 0.0 copy-start.3
  1201.3 0.6 multiply_reduce_fusion.1
  1201.9 1.4 copy-done.3
  1203.3 0.9 add_convert_fusion.1
  1204.2 1.3 convolution_bitcast_fusion
  1205.5 1.3 convolution_bitcast_fusion.1
  1206.8 3.8 fusion.4
  1210.6 3.9 copy.73
  1214.5 0.0 all-gather.5.cloned.1.call-update
  1214.5 4.3 copy.69
  1218.8 7.2 all-to-all-start
  1226.0 2.8 fusion.38
  1228.8 47.6 %all-to-all-done = bf16[128,8,1024]{0,1,2:T(8,128)(2,1)} async-done(((bf16[128,8,1024]{0,1,2:T(8,128)(2,1)}), bf16[128,8,1024]{0,1,2:T(8,128)(2,1)}, u32[]{:S(2)}, u32[]{:S(2)}) %all-to-all-start) | async-done | bytes 2097184 | tf_op jit(solution)/shard_map/all_to_all | solution.py:46
  1276.5 3.6 copy.71
  1280.0 3.7 copy.74
  1283.8 476.1 %all-gather.5.cloned.1.call-done = bf16[128,1024,1024]{2,0,1:T(8,128)(2,1)} async-done(((bf16[128,8,1024]{2,0,1:T(8,128)(2,1)}), bf16[128,1024,1024]{2,0,1:T(8,128)(2,1)}) %all-gather.5.cloned.1.call-update) | async-done | bytes 268435456 | tf_op jit(solution)/shard_map/all_gather | solution.py:47
  1759.8 424.9 %fusion.46 = (f32[8,1024]{1,0:T(8,128)S(1)}, f32[128,8,1024]{2,1,0:T(8,128)}) fusion(bf16[128,1024,8]{1,2,0:T(8,128)(2,1)S(1)} %copy.74, bf16[128,1024,1024]{2,0,1:T(8,128)(2,1)} %all-gather.5.cloned.1.call-done), kind=kOutput, calls=%fused_computation.84 | convolution fusion | flops 2148524032 | bytes 274759680 | tf_op jit(solution)/shard_map/cki,ckj->cij/dot_general | solution.py:48
  2184.7 0.0 copy-start.1
  2184.7 0.0 copy-start.13
  2184.8 0.0 copy-start.14
  2184.8 2.8 multiply_reduce_fusion
  2187.6 0.6 copy-done.1
  2188.2 0.0 copy-done.13
  2188.2 0.0 copy-done.14
  2188.2 0.6 add_convert_fusion
  2188.8 1.1 copy-done.4
  2189.9 6.6 multiply_add_fusion
  2196.5 5.3 copy.78
  (16 shorter events, 0.1 us)
Async XLA Ops:
  6.5 7.6 copy-start.10
  6.5 7.6 copy-start.9
  6.5 550.3 %all-gather.3.cloned.1.call-start = ((), (), s32[]{:S(2)}) async-start(), calls=%async_computation.1 | async-start | bytes 270532608 | tf_op jit(solution)/shard_map/all_gather | solution.py:40
  9.9 4.2 copy-start
  14.1 3.0 copy-start.6
  18.3 1.3 copy-start.8
  27.3 1732.5 %all-gather.5.cloned.1.call-start = ((), (), s32[]{:S(2)}) async-start(), calls=%async_computation.2 | async-start | bytes 270532608 | tf_op jit(solution)/shard_map/all_gather | solution.py:47
  32.7 4.3 copy-start.11
  32.7 4.3 copy-start.12
  32.7 4.8 copy-start.7
  1190.5 3.5 copy-start.2
  1193.4 2.3 copy-start.5
  1193.4 2.3 copy-start.15
  1201.3 2.0 copy-start.3
  1218.8 57.7 %all-to-all-start = ((bf16[128,8,1024]{0,1,2:T(8,128)(2,1)}), bf16[128,8,1024]{0,1,2:T(8,128)(2,1)}, u32[]{:S(2)}, u32[]{:S(2)}) async-start(bf16[128,8,1024]{0,1,2:T(8,128)(2,1)} %copy.69), calls=%async_computation | async-start | bytes 4194304 | tf_op jit(solution)/shard_map/all_to_all | solution.py:46
  2184.7 3.5 copy-start.1
  2184.7 3.4 copy-start.13
  2184.8 3.4 copy-start.14
  2187.6 2.3 copy-start.4
Sparse Core Ops, SparseCore 0:
  27.4 529.3 all-gather.2
  1214.6 545.1 all-gather.4
where the time goes:
time: 2220 us; the launch traced here: 2210 us
  matrix products  1080 us (49%)
  waiting for transfers between devices  1040 us (47%)
  local copies, waits for them, and re-layouts  39 us (2%)
  other arithmetic  27.1 us (1%)
    all_gather x2, waiting for transfers between devices, local_step(): full_b = lax.all_gather(side_b, GROUP_AXES, axis=1, tiled=True)  993 us
    dot_general x1, matrix products, local_step(): jnp.einsum('cik,cjk->cij', side_a, full_b, preferred_element_type=jnp.flo...  634 us
    dot_general x1, matrix products, local_step(): jnp.einsum('cki,ckj->cij', cols_a, full_b, preferred_element_type=jnp.flo...  425 us
    all_to_all x1, waiting for transfers between devices, local_step(): cols_a = lax.all_to_all(side_a, GROUP_AXES, 2, 1, tiled=True)  47.6 us
  transfers between devices with their start and end apart: 3, of which 3 were waited for; matrix products, arithmetic and copies ran while one was open for 1% of the time, Pallas kernels for 0%

commit v1 on v0

v1 whole, which is shorter than its diff:
```python
import jax
import jax.numpy as jnp
from jax import lax
from jax.experimental import pallas as pl
from jax.experimental.pallas import tpu as pltpu
from jax.sharding import PartitionSpec as P

NORM_EPS = 1e-5
ROW_SPEC = P(('data', 'dap2', 'dap'), None, None)
MASK_SPEC = P(('data', 'dap2', 'dap'), None)

N = 1024
C = 128
ROWS = 8
LANES = 128
BLOCKS = N // LANES
CHUNKS = 4
PER = BLOCKS // CHUNKS


def norm_t(values, gain, bias):
    mean = jnp.sum(values, axis=0, keepdims=True) * (1.0 / C)
    centered = values - mean
    var = jnp.sum(centered * centered, axis=0, keepdims=True) * (1.0 / C)
    return (centered * lax.rsqrt(var + NORM_EPS) * gain + bias).astype(jnp.bfloat16)


def body(z_ref, mask_ref, wproj_ref, wgate_ref, wout_ref, vec_ref, out_ref,
         y_ref, g_ref, yn_ref, stage_ref, sab_ref, rab0_ref, rab1_ref, sx_ref, rx0_ref, rx1_ref, a_ref, b_ref,
         ssem, rsem):
    d2 = lax.axis_index('dap2')
    d1 = lax.axis_index('dap')
    me = d2 * 8 + d1
    mz, my, mx, mc = lax.div(d2, 4), lax.rem(d2, 4), lax.div(d1, 2), lax.rem(d1, 2)
    lines = [lax.rem(mx + dx, 4) * 2 + lax.rem(mc + dc, 2) for dx in range(4) for dc in range(2)]

    def everyone(fn):
        @pl.loop(0, 16)
        def _(o):
            t2 = lax.rem(mz + lax.div(o, 4), 4) * 4 + lax.rem(my + lax.rem(o, 4), 4)
            for n in range(1, 8):
                fn(t2, lines[n])

            @pl.when(o != 0)
            def _():
                fn(t2, lines[0])

    barrier = pltpu.get_barrier_semaphore()
    everyone(lambda t2, t1: pl.semaphore_signal(
        barrier, 1, device_id={'dap2': t2, 'dap': t1}, device_id_type=pl.DeviceIdType.MESH))

    def send(src_of, dst, kind, q):
        everyone(lambda t2, t1: pltpu.make_async_remote_copy(
            src_of(t2 * 8 + t1), dst, ssem.at[kind, q], rsem.at[kind, q],
            device_id={'dap2': t2, 'dap': t1}, device_id_type=pl.DeviceIdType.MESH).start())

    def arrival(ref, kind, q):
        return pltpu.make_async_remote_copy(ref, ref, ssem.at[kind, q], rsem.at[kind, q],
                                            device_id={'dap2': d2, 'dap': d1},
                                            device_id_type=pl.DeviceIdType.MESH)

    def lanes_of(kb):
        return pl.ds(pl.multiple_of(kb * LANES, LANES), LANES)

    def project(s, y, r, lanes):
        yn = norm_t(y, vec_ref[s, 0], vec_ref[s, 1])
        yn_ref[r, :, lanes] = yn
        keep = mask_ref[r, :, lanes].astype(jnp.float32)
        for side in range(2):
            p = jnp.dot(wproj_ref[s, 2 * C * side:2 * C * (side + 1), :], yn, preferred_element_type=jnp.float32)
            stage_ref[side, pl.ds(r, C, stride=ROWS), :] = keep * jax.nn.sigmoid(p[C:]) * p[:C]

    def pack(kb):
        sides = [stage_ref[side].reshape(C, ROWS, LANES) for side in range(2)]
        sab_ref[kb] = jnp.concatenate(sides, axis=1).astype(jnp.bfloat16)

    def gates(s):
        @pl.loop(0, BLOCKS)
        def _(kb):
            @pl.loop(0, ROWS)
            def _(r):
                pre = jnp.dot(wgate_ref[s], yn_ref[r, :, lanes_of(kb)], preferred_element_type=jnp.float32)
                g_ref[r, :, lanes_of(kb)] = jax.nn.sigmoid(pre)

    def send_sides(q, rab_ref, kind):
        blocks = pl.ds(q * PER, PER)
        send(lambda t: sab_ref.at[blocks, t], rab_ref.at[blocks, me], kind, q)
        rab_ref[blocks, me] = sab_ref[blocks, me]

    def send_mix(q, rx_ref, kind):
        blocks = pl.ds(q * PER, PER)
        send(lambda t: sx_ref.at[blocks, pl.ds(pl.multiple_of(t * ROWS, ROWS), ROWS)],
             rx_ref.at[blocks, pl.ds(pl.multiple_of(me * ROWS, ROWS), ROWS)], kind, q)
        own = pl.ds(pl.multiple_of(me * ROWS, ROWS), ROWS)
        rx_ref[blocks, own] = sx_ref[blocks, own]

    def wait_sides(q, rab_ref, kind):
        arrival(rab_ref.at[pl.ds(q * PER, PER), pl.ds(0, C - 1)], kind, q).wait_recv()

    def wait_mix(q, rx_ref, kind):
        arrival(rx_ref.at[pl.ds(q * PER, PER), pl.ds(0, N - ROWS)], kind, q).wait_recv()

    def drain(kind, q):
        if kind in (0, 2):
            arrival(sab_ref.at[pl.ds(q * PER, PER), pl.ds(0, C - 1)], kind, q).wait_send()
        else:
            arrival(sx_ref.at[pl.ds(q * PER, PER), pl.ds(0, N - ROWS)], kind, q).wait_send()

    def update_of(s, rx_ref, kb, r):
        lanes = lanes_of(kb)
        xn = norm_t(rx_ref[kb, pl.ds(r, C, stride=ROWS), :], vec_ref[s, 2], vec_ref[s, 3])
        upd = jnp.dot(wout_ref[s], xn, preferred_element_type=jnp.float32)
        return y_ref[r, :, lanes] + g_ref[r, :, lanes] * upd

    @pl.loop(0, CHUNKS)
    def _(q):
        @pl.loop(q * PER, (q + 1) * PER)
        def _(kb):
            @pl.loop(0, ROWS)
            def _(r):
                y = z_ref[r, lanes_of(kb), :].T
                y_ref[r, :, lanes_of(kb)] = y
                project(0, y, r, lanes_of(kb))
            pack(kb)

        @pl.when(q == 0)
        def _():
            pl.semaphore_wait(barrier, 127)
        send_sides(q, rab0_ref, 0)
    gates(0)

    @pl.loop(0, CHUNKS)
    def _(q):
        wait_sides(q, rab0_ref, 0)

        @pl.loop(q * PER, (q + 1) * PER)
        def _(kb):
            both = rab0_ref[kb].astype(jnp.float32)
            a_ref[:, lanes_of(kb)] = both[:, :ROWS].reshape(N, LANES).astype(jnp.bfloat16)
            b_ref[:, lanes_of(kb)] = both[:, ROWS:].reshape(N, LANES).astype(jnp.bfloat16)

    @pl.loop(0, CHUNKS)
    def _(q):
        @pl.loop(q * PER, (q + 1) * PER)
        def _(jb):
            rows = b_ref[pl.ds(pl.multiple_of(jb * LANES, LANES), LANES), :]
            sx_ref[jb] = lax.dot_general(a_ref[...], rows, (((1,), (1,)), ((), ())),
                                         preferred_element_type=jnp.float32)
        send_mix(q, rx0_ref, 1)

    @pl.loop(0, CHUNKS)
    def _(q):
        drain(0, q)
    @pl.loop(0, CHUNKS)
    def _(q):
        wait_mix(q, rx0_ref, 1)

        @pl.loop(q * PER, (q + 1) * PER)
        def _(kb):
            @pl.loop(0, ROWS)
            def _(r):
                y = update_of(0, rx0_ref, kb, r)
                y_ref[r, :, lanes_of(kb)] = y
                project(1, y, r, lanes_of(kb))
            pack(kb)
        send_sides(q, rab1_ref, 2)
    gates(1)

    @pl.loop(0, CHUNKS)
    def _(q):
        drain(1, q)
    @pl.loop(0, CHUNKS)
    def _(q):
        wait_sides(q, rab1_ref, 2)

        @pl.loop(q * PER, (q + 1) * PER)
        def _(kb):
            both = rab1_ref[kb].astype(jnp.float32)
            a_ref[pl.ds(pl.multiple_of(kb * LANES, LANES), LANES), :] = (
                both[:, :ROWS].reshape(N, LANES).T.astype(jnp.bfloat16))
            b_ref[:, lanes_of(kb)] = both[:, ROWS:].reshape(N, LANES).astype(jnp.bfloat16)

    @pl.loop(0, CHUNKS)
    def _(q):
        @pl.loop(q * PER, (q + 1) * PER)
        def _(jb):
            sx_ref[jb] = jnp.dot(a_ref[...], b_ref[:, lanes_of(jb)], preferred_element_type=jnp.float32)
        send_mix(q, rx1_ref, 3)

    @pl.loop(0, CHUNKS)
    def _(q):
        wait_mix(q, rx1_ref, 3)

        @pl.loop(q * PER, (q + 1) * PER)
        def _(kb):
            @pl.loop(0, ROWS)
            def _(r):
                out_ref[r, lanes_of(kb), :] = update_of(1, rx1_ref, kb, r).T

    @pl.loop(0, CHUNKS)
    def _(q):
        drain(2, q)
        drain(3, q)


def solution(mesh):
    def local_step(pair_rows, mask_rows, norm_gain, norm_bias, w_proj, w_gate, post_gain, post_bias, w_out):
        vecs = jnp.stack([norm_gain, norm_bias, post_gain, post_bias], axis=1).astype(jnp.float32)
        vecs = jnp.broadcast_to(vecs[..., None], vecs.shape + (LANES,))
        turned = [jnp.swapaxes(w, 1, 2) for w in (w_proj, w_gate, w_out)]
        vmem = pl.BlockSpec(memory_space=pltpu.VMEM)
        sides = pltpu.VMEM((BLOCKS, C, 2 * ROWS, LANES), jnp.bfloat16)
        mix = pltpu.VMEM((BLOCKS, N, LANES), jnp.float32)
        rows = pltpu.VMEM((ROWS, C, N), jnp.float32)
        square = pltpu.VMEM((N, N), jnp.bfloat16)
        return pl.pallas_call(
            body,
            name='triangle_pair',
            out_shape=jax.ShapeDtypeStruct(pair_rows.shape, jnp.float32),
            in_specs=[vmem] * 6,
            out_specs=vmem,
            scratch_shapes=[rows, rows, pltpu.VMEM((ROWS, C, N), jnp.bfloat16),
                            pltpu.VMEM((2, N, LANES), jnp.float32),
                            sides, sides, sides, mix, mix, mix, square, square,
                            pltpu.SemaphoreType.DMA((4, CHUNKS)), pltpu.SemaphoreType.DMA((4, CHUNKS))],
            compiler_params=pltpu.CompilerParams(collective_id=0, has_side_effects=True,
                                                 vmem_limit_bytes=66_000_000),
        )(pair_rows, mask_rows[:, None], *turned, vecs)

    replicated = P()
    return jax.shard_map(local_step, mesh=mesh,
                         in_specs=(ROW_SPEC, MASK_SPEC) + (replicated,) * 7,
                         out_specs=ROW_SPEC, check_vma=False)
```

time: 2220 us -> 251 us (0.11)
  matrix products: 1080 us -> 0 us
  waiting for transfers between devices: 1040 us -> 0 us
  Pallas kernels: 0 us -> 233 us
  other arithmetic: 27.1 us -> 0.01 us
  local copies, waits for them, and re-layouts: 39 us -> 14.4 us
    dot_general x10 -> x0, matrix products: 1080 us -> none  [the longest x1 634 us: local_step(): jnp.einsum('cik,cjk->cij', side_a, full_b, preferred_element_type=jnp.flo...]
    all_gather x2 -> x0, waiting for transfers between devices: 993 us -> none  [local_step(): full_b = lax.all_gather(side_b, GROUP_AXES, axis=1, tiled=True)]
    pallas_call x0 -> x1, Pallas kernels: none -> 233 us  [local_step(): pl.pallas_call(body, name='triangle_pair', out_shape=jax.ShapeDtypeStruct...]
    all_to_all x1 -> x0, waiting for transfers between devices: 47.6 us -> none  [local_step(): cols_a = lax.all_to_all(side_a, GROUP_AXES, 2, 1, tiled=True)]
  transfers between devices with their start and end apart: 3 -> 0, of which waited for: 3 -> 0; matrix products, arithmetic and copies ran while one was open for 1% -> 0% of each run, Pallas kernels for 0% -> 0%
where the time goes in v1:
time: 251 us; the launch traced here: 247 us
  Pallas kernels  233 us (93%)
  local copies, waits for them, and re-layouts  14.4 us (6%)
    pallas_call x1, Pallas kernels, local_step(): pl.pallas_call(body, name='triangle_pair', out_shape=jax.ShapeDtypeStruct...  233 us
    unnamed x4, local copies, waits for them, and re-layouts  9.39 us

profile of v1, /device:TPU:1, one launch (start us, length us, event | category | flops | bytes accessed | tf_op | source)
XLA Modules:
  0.0 247.1 jit_solution(7683114399042324467)
XLA Ops:
  0.0 0.7 copy.20
  0.7 0.7 copy.21
  1.3 0.7 copy.22
  2.0 0.7 copy.23
  2.6 1.4 broadcast_in_dim.4.mask_ref
  4.0 1.6 copy.18
  5.6 1.6 copy.19
  7.1 1.8 copy.17
  8.9 1.0 broadcast_in_dim.10.vec_ref
  9.9 232.7 %triangle_pair.1 = f32[8,1024,128]{2,1,0:T(8,128)} custom-call(f32[8,1024,128]{2,1,0:T(8,128)} %z_ref.1, s32[8,1,1024]{2,1,0:T(1,128)} %broadcast_in_dim.4.mask_ref, bf16[2,512,128]{2,1,0:T(8,128)(2,1)} %bitcast.7, bf16[2,128,128]{2,1,0:T(8,128)(2,1)} %bitcast.8, bf16[2,128,128]{2,1,0:T(8,128)(2,1)} %bitcast.9, f32[2,4,128,128]{3,2,1,0:T(8,128)} %broadcast_in_dim.10.vec_ref), custom_call_target="tpu_custom_call" | custom-call | tf_op jit(solution)/shard_map/triangle_pair/pallas_call | solution.py:216
  242.6 4.5 %copy.25 = f32[8,1024,128]{2,1,0:T(8,128)} copy(f32[8,1024,128]{2,1,0:T(8,128)} %triangle_pair.1) | data formatting | bytes 8388608
  (1 shorter events, 0.0 us)

commit v2 on v1

v2 whole, which is shorter than its diff:
```python
import jax
import jax.numpy as jnp
from jax import lax
from jax.experimental import pallas as pl
from jax.experimental.pallas import tpu as pltpu
from jax.sharding import PartitionSpec as P

NORM_EPS = 1e-5
ROW_SPEC = P(('data', 'dap2', 'dap'), None, None)
MASK_SPEC = P(('data', 'dap2', 'dap'), None)

N = 1024
C = 128
ROWS = 8
LANES = 128
BLOCKS = N // LANES
CHUNKS = 4
PER = BLOCKS // CHUNKS
WIDE = PER * LANES
UNROLL = 2


def partner_offsets():
    kinds = {}
    for z in range(4):
        for y in range(4):
            for x in range(4):
                kinds.setdefault(tuple(sorted(min(v, 4 - v) for v in (z, y, x))), []).append((z, y, x))
    offsets = []
    for kind in sorted(kinds, key=lambda k: (-sum(k), k)):
        group = []
        for first in kinds[kind]:
            for turn in range(3):
                turned = first[turn:] + first[:turn]
                for entry in (turned, tuple((4 - v) % 4 for v in turned)):
                    if entry not in group:
                        group.append(entry)
        for core in range(2):
            offsets += [entry + (core,) for entry in group if entry + (core,) != (0, 0, 0, 0)]
    return offsets


OFFSETS = partner_offsets()


def norm_t(values, gain, bias):
    mean = jnp.sum(values, axis=0, keepdims=True) * (1.0 / C)
    centered = values - mean
    var = jnp.sum(centered * centered, axis=0, keepdims=True) * (1.0 / C)
    return (centered * lax.rsqrt(var + NORM_EPS) * gain + bias).astype(jnp.bfloat16)


def scoped(name, fn, *args):
    with jax.named_scope(name):
        return fn(*args)


def body(z_hbm, mask_ref, ngain_ref, nbias_ref, wproj_in, wgate_in, pgain_ref, pbias_ref, wout_in, out_hbm,
         z_ref, keep_ref, wproj_ref, wgate_ref, wout_ref, vec_ref,
         y_ref, g_ref, yn_ref, stage_ref, sab_ref, rab0_ref, rab1_ref, sx_ref, rx0_ref, rx1_ref, a_ref, b_ref,
         ssem, rsem, zsem, osem):
    def z_copy(q):
        cols = pl.ds(pl.multiple_of(q * WIDE, WIDE), WIDE)
        return pltpu.make_async_copy(z_hbm.at[:, cols], z_ref.at[:, cols], zsem.at[q])

    def out_copy(q):
        cols = pl.ds(pl.multiple_of(q * WIDE, WIDE), WIDE)
        return pltpu.make_async_copy(z_ref.at[:, cols], out_hbm.at[:, cols], osem.at[q])

    for q in range(CHUNKS):
        z_copy(q).start()

    d2 = lax.axis_index('dap2')
    d1 = lax.axis_index('dap')
    me = d2 * 8 + d1
    mz, my, mx, mc = lax.div(d2, 4), lax.rem(d2, 4), lax.div(d1, 2), lax.rem(d1, 2)
    lines = {(dx, dc): lax.rem(mx + dx, 4) * 2 + lax.rem(mc + dc, 2) for dx in range(4) for dc in range(2)}
    planes = {(dz, dy): lax.rem(mz + dz, 4) * 4 + lax.rem(my + dy, 4) for dz in range(4) for dy in range(4)}

    def everyone(fn):
        for dz, dy, dx, dc in OFFSETS:
            fn(planes[dz, dy], lines[dx, dc])

    barrier = pltpu.get_barrier_semaphore()
    everyone(lambda t2, t1: pl.semaphore_signal(
        barrier, 1, device_id={'dap2': t2, 'dap': t1}, device_id_type=pl.DeviceIdType.MESH))

    def send(src_of, dst, kind, q):
        everyone(lambda t2, t1: pltpu.make_async_remote_copy(
            src_of(t2 * 8 + t1), dst, ssem.at[kind, q], rsem.at[kind, q],
            device_id={'dap2': t2, 'dap': t1}, device_id_type=pl.DeviceIdType.MESH).start())

    def arrival(ref, kind, q):
        return pltpu.make_async_remote_copy(ref, ref, ssem.at[kind, q], rsem.at[kind, q],
                                            device_id={'dap2': d2, 'dap': d1},
                                            device_id_type=pl.DeviceIdType.MESH)

    def lanes_of(kb):
        return pl.ds(pl.multiple_of(kb * LANES, LANES), LANES)

    def wide_of(q):
        return pl.ds(pl.multiple_of(q * WIDE, WIDE), WIDE)

    def vec(s, n):
        return jnp.concatenate([vec_ref[s, n]] * PER, axis=1)

    def project(s, y, r, q):
        yn = norm_t(y, vec(s, 0), vec(s, 1))
        yn_ref[r, :, wide_of(q)] = yn
        keep = keep_ref[r, :, wide_of(q)]
        for side in range(2):
            p = jnp.dot(wproj_ref[s, 2 * C * side:2 * C * (side + 1), :], yn, preferred_element_type=jnp.float32)
            part = keep * jax.nn.sigmoid(p[C:]) * p[:C]
            for n in range(PER):
                stage_ref[side, n, pl.ds(r, C, stride=ROWS), :] = part[:, n * LANES:(n + 1) * LANES]

    def column(ref, s):
        return jnp.broadcast_to(ref[...].astype(jnp.float32)[s:s + 1], (C, LANES)).T

    def turn(ref, s, lo):
        return ref[s, :, lo:lo + C].astype(jnp.float32).T.astype(jnp.bfloat16)

    def set_up_norm(s):
        vec_ref[s, 0] = column(ngain_ref, s)
        vec_ref[s, 1] = column(nbias_ref, s)
        for n in range(4):
            wproj_ref[s, n * C:(n + 1) * C] = turn(wproj_in, s, n * C)

    def set_up_rest(s):
        vec_ref[s, 2] = column(pgain_ref, s)
        vec_ref[s, 3] = column(pbias_ref, s)
        wgate_ref[s] = turn(wgate_in, s, 0)
        wout_ref[s] = turn(wout_in, s, 0)

    def pack(q):
        for n in range(PER):
            sides = [stage_ref[side, n].reshape(C, ROWS, LANES) for side in range(2)]
            sab_ref[q * PER + n] = jnp.concatenate(sides, axis=1).astype(jnp.bfloat16)

    def gates(s):
        @pl.loop(0, CHUNKS)
        def _(q):
            @pl.loop(0, ROWS, unroll=2)
            def _(r):
                pre = jnp.dot(wgate_ref[s], yn_ref[r, :, wide_of(q)], preferred_element_type=jnp.float32)
                g_ref[r, :, wide_of(q)] = jax.nn.sigmoid(pre)

    def send_sides(q, rab_ref, kind):
        blocks = pl.ds(q * PER, PER)
        send(lambda t: sab_ref.at[blocks, t], rab_ref.at[blocks, me], kind, q)
        rab_ref[blocks, me] = sab_ref[blocks, me]

    def send_mix(q, rx_ref, kind):
        blocks = pl.ds(q * PER, PER)
        send(lambda t: sx_ref.at[blocks, pl.ds(pl.multiple_of(t * ROWS, ROWS), ROWS)],
             rx_ref.at[blocks, pl.ds(pl.multiple_of(me * ROWS, ROWS), ROWS)], kind, q)
        own = pl.ds(pl.multiple_of(me * ROWS, ROWS), ROWS)
        rx_ref[blocks, own] = sx_ref[blocks, own]

    def wait_sides(q, rab_ref, kind):
        arrival(rab_ref.at[pl.ds(q * PER, PER), pl.ds(0, C - 1)], kind, q).wait_recv()

    def wait_mix(q, rx_ref, kind):
        arrival(rx_ref.at[pl.ds(q * PER, PER), pl.ds(0, N - ROWS)], kind, q).wait_recv()

    def drain(kind, q):
        if kind in (0, 2):
            arrival(sab_ref.at[pl.ds(q * PER, PER), pl.ds(0, C - 1)], kind, q).wait_send()
        else:
            arrival(sx_ref.at[pl.ds(q * PER, PER), pl.ds(0, N - ROWS)], kind, q).wait_send()

    def update_of(s, rx_ref, q, r):
        x = jnp.concatenate([rx_ref[q * PER + n, pl.ds(r, C, stride=ROWS), :] for n in range(PER)], axis=1)
        xn = norm_t(x, vec(s, 2), vec(s, 3))
        upd = jnp.dot(wout_ref[s], xn, preferred_element_type=jnp.float32)
        return y_ref[r, :, wide_of(q)] + g_ref[r, :, wide_of(q)] * upd

    for r in range(ROWS):
        keep_ref[r] = mask_ref[r:r + 1, :].astype(jnp.float32)
    set_up_norm(0)

    @pl.loop(0, CHUNKS)
    def _(q):
        z_copy(q).wait()

        @pl.loop(0, ROWS, unroll=UNROLL)
        def _(r):
            y = z_ref[r, wide_of(q), :].T
            y_ref[r, :, wide_of(q)] = y
            project(0, y, r, q)
        pack(q)

        @pl.when(q == 0)
        def _():
            scoped('entry', pl.semaphore_wait, barrier, 127)
        scoped('send_s0', send_sides, q, rab0_ref, 0)
    set_up_rest(0)
    set_up_norm(1)
    set_up_rest(1)
    scoped('gates', gates, 0)

    @pl.loop(0, CHUNKS)
    def _(q):
        scoped('wait_s0', wait_sides, q, rab0_ref, 0)

        @pl.loop(q * PER, (q + 1) * PER)
        def _(kb):
            both = rab0_ref[kb].astype(jnp.float32)
            a_ref[:, lanes_of(kb)] = both[:, :ROWS].reshape(N, LANES).astype(jnp.bfloat16)
            b_ref[:, lanes_of(kb)] = both[:, ROWS:].reshape(N, LANES).astype(jnp.bfloat16)

    @pl.loop(0, CHUNKS)
    def _(q):
        @pl.loop(q * PER, (q + 1) * PER)
        def _(jb):
            rows = b_ref[pl.ds(pl.multiple_of(jb * LANES, LANES), LANES), :]
            sx_ref[jb] = lax.dot_general(a_ref[...], rows, (((1,), (1,)), ((), ())),
                                         preferred_element_type=jnp.float32)
        scoped('send_m0', send_mix, q, rx0_ref, 1)

    @pl.loop(0, CHUNKS)
    def _(q):
        drain(0, q)
    @pl.loop(0, CHUNKS)
    def _(q):
        scoped('wait_m0', wait_mix, q, rx0_ref, 1)

        @pl.loop(0, ROWS, unroll=UNROLL)
        def _(r):
            y = update_of(0, rx0_ref, q, r)
            y_ref[r, :, wide_of(q)] = y
            project(1, y, r, q)
        pack(q)
        scoped('send_s1', send_sides, q, rab1_ref, 2)
    scoped('gates', gates, 1)

    @pl.loop(0, CHUNKS)
    def _(q):
        drain(1, q)
    @pl.loop(0, CHUNKS)
    def _(q):
        scoped('wait_s1', wait_sides, q, rab1_ref, 2)

        @pl.loop(q * PER, (q + 1) * PER)
        def _(kb):
            both = rab1_ref[kb].astype(jnp.float32)
            a_ref[pl.ds(pl.multiple_of(kb * LANES, LANES), LANES), :] = (
                both[:, :ROWS].reshape(N, LANES).T.astype(jnp.bfloat16))
            b_ref[:, lanes_of(kb)] = both[:, ROWS:].reshape(N, LANES).astype(jnp.bfloat16)

    @pl.loop(0, CHUNKS)
    def _(q):
        @pl.loop(q * PER, (q + 1) * PER)
        def _(jb):
            sx_ref[jb] = jnp.dot(a_ref[...], b_ref[:, lanes_of(jb)], preferred_element_type=jnp.float32)
        scoped('send_m1', send_mix, q, rx1_ref, 3)

    @pl.loop(0, CHUNKS)
    def _(q):
        scoped('wait_m1', wait_mix, q, rx1_ref, 3)

        @pl.loop(0, ROWS, unroll=UNROLL)
        def _(r):
            z_ref[r, wide_of(q), :] = update_of(1, rx1_ref, q, r).T
        out_copy(q).start()

    @pl.loop(0, CHUNKS)
    def _(q):
        drain(2, q)
        drain(3, q)
        out_copy(q).wait()


def solution(mesh):
    def local_step(*args):
        vmem = pl.BlockSpec(memory_space=pltpu.VMEM)
        hbm = pl.BlockSpec(memory_space=pl.ANY)
        f32, bf16 = jnp.float32, jnp.bfloat16
        sides = pltpu.VMEM((BLOCKS, C, 2 * ROWS, LANES), bf16)
        mix = pltpu.VMEM((BLOCKS, N, LANES), f32)
        rows = pltpu.VMEM((ROWS, C, N), f32)
        square = pltpu.VMEM((N, N), bf16)
        exchange = pltpu.SemaphoreType.DMA((4, CHUNKS))
        chunk = pltpu.SemaphoreType.DMA((CHUNKS,))
        return pl.pallas_call(
            body,
            name='triangle_pair',
            out_shape=jax.ShapeDtypeStruct((ROWS, N, C), f32),
            in_specs=[hbm] + [vmem] * 8,
            out_specs=hbm,
            scratch_shapes=[pltpu.VMEM((ROWS, N, C), f32), pltpu.VMEM((ROWS, 1, N), f32),
                            pltpu.VMEM((2, 4 * C, C), bf16), pltpu.VMEM((2, C, C), bf16),
                            pltpu.VMEM((2, C, C), bf16), pltpu.VMEM((2, 4, C, LANES), f32),
                            rows, rows, pltpu.VMEM((ROWS, C, N), bf16), pltpu.VMEM((2, PER, N, LANES), f32),
                            sides, sides, sides, mix, mix, mix, square, square,
                            exchange, exchange, chunk, chunk],
            compiler_params=pltpu.CompilerParams(collective_id=0, has_side_effects=True,
                                                 vmem_limit_bytes=66_000_000),
        )(*args)

    replicated = P()
    return jax.shard_map(local_step, mesh=mesh,
                         in_specs=(ROW_SPEC, MASK_SPEC) + (replicated,) * 7,
                         out_specs=ROW_SPEC, check_vma=False)
```

time: 251 us -> 236 us (0.940)
  the two profiles are of different devices: /device:TPU:1 before, /device:TPU:11 now
where the time goes in v2:
time: 236 us
  Pallas kernels  231 us (98%)
  local copies, waits for them, and re-layouts  4.5 us (2%)
    pallas_call x1, Pallas kernels, local_step(): pl.pallas_call(body, name='triangle_pair', out_shape=jax.ShapeDtypeStruct...  231 us

profile of v2, /device:TPU:11, one launch (start us, length us, event | category | flops | bytes accessed | tf_op | source)
XLA Modules:
  0.0 235.7 jit_solution(8216618404315383943)
XLA Ops:
  0.0 231.2 %triangle_pair.1 = f32[8,1024,128]{2,1,0:T(8,128)} custom-call(f32[8,1024,128]{2,1,0:T(8,128)} %z_hbm.1, s32[8,1024]{1,0:T(8,128)} %mask_ref.1, bf16[2,128]{1,0:T(2,128)(2,1)} %ngain_ref.1, bf16[2,128]{1,0:T(2,128)(2,1)} %nbias_ref.1, bf16[2,128,512]{2,1,0:T(8,128)(2,1)} %wproj_in.1, bf16[2,128,128]{2,1,0:T(8,128)(2,1)} %wgate_in.1, ...), custom_call_target="tpu_custom_call" | custom-call | tf_op jit(solution)/shard_map/triangle_pair/pallas_call | solution.py:285
  231.2 4.5 %copy.11 = f32[8,1024,128]{2,1,0:T(8,128)} copy(f32[8,1024,128]{2,1,0:T(8,128)} %triangle_pair.1) | data formatting | bytes 8388608

commit v3 on v2

--- a/solution.py
+++ b/solution.py
@@ -1,3 +1,5 @@
+import random
+
 import jax
 import jax.numpy as jnp
 from jax import lax
@@ -14,29 +16,15 @@
 ROWS = 8
 LANES = 128
 BLOCKS = N // LANES
-CHUNKS = 4
+CHUNKS = 8
 PER = BLOCKS // CHUNKS
 WIDE = PER * LANES
 UNROLL = 2
 
 
 def partner_offsets():
-    kinds = {}
-    for z in range(4):
-        for y in range(4):
-            for x in range(4):
-                kinds.setdefault(tuple(sorted(min(v, 4 - v) for v in (z, y, x))), []).append((z, y, x))
-    offsets = []
-    for kind in sorted(kinds, key=lambda k: (-sum(k), k)):
-        group = []
-        for first in kinds[kind]:
-            for turn in range(3):
-                turned = first[turn:] + first[:turn]
-                for entry in (turned, tuple((4 - v) % 4 for v in turned)):
-                    if entry not in group:
-                        group.append(entry)
-        for core in range(2):
-            offsets += [entry + (core,) for entry in group if entry + (core,) != (0, 0, 0, 0)]
+    offsets = [(z, y, x, c) for z in range(4) for y in range(4) for x in range(4) for c in range(2)][1:]
+    random.Random(0).shuffle(offsets)
     return offsets
 
 

time: 236 us -> 212 us (0.90)
  the two profiles are of different devices: /device:TPU:11 before, /device:TPU:1 now
where the time goes in v3:
time: 212 us
  Pallas kernels  208 us (98%)
  local copies, waits for them, and re-layouts  4.5 us (2%)
    pallas_call x1, Pallas kernels, local_step(): pl.pallas_call(body, name='triangle_pair', out_shape=jax.ShapeDtypeStruct...  208 us
    unnamed x1, local copies, waits for them, and re-layouts  4.5 us

profile of v3, /device:TPU:1, one launch (start us, length us, event | category | flops | bytes accessed | tf_op | source)
XLA Modules:
  0.0 212.1 jit_solution(10516106771571017726)
XLA Ops:
  0.0 207.6 %triangle_pair.1 = f32[8,1024,128]{2,1,0:T(8,128)} custom-call(f32[8,1024,128]{2,1,0:T(8,128)} %z_hbm.1, s32[8,1024]{1,0:T(8,128)} %mask_ref.1, bf16[2,128]{1,0:T(2,128)(2,1)} %ngain_ref.1, bf16[2,128]{1,0:T(2,128)(2,1)} %nbias_ref.1, bf16[2,128,512]{2,1,0:T(8,128)(2,1)} %wproj_in.1, bf16[2,128,128]{2,1,0:T(8,128)(2,1)} %wgate_in.1, ...), custom_call_target="tpu_custom_call" | custom-call | tf_op jit(solution)/shard_map/triangle_pair/pallas_call | solution.py:273
  207.6 4.5 %copy.11 = f32[8,1024,128]{2,1,0:T(8,128)} copy(f32[8,1024,128]{2,1,0:T(8,128)} %triangle_pair.1) | data formatting | bytes 8388608
